TPU v7x, 512 devices: a whole 4x8x8 slice. The times are simulated.
512 devices in a mesh: row: 16 (over x_hi, z), col: 32 (over y, x_lo, core).
Axes of the slice: x: 4 (x_hi: 2, x_lo: 2; x = x_hi * 2 + x_lo), y: 8, z: 8, core: 2. Of those that a mesh axis runs over, the one named last changes fastest.
Arguments:
- raw_records: bfloat16 [2048, 768], P(('row', 'col')), may hold values from -6 to 6
- filter_taps: float32 [129], replicated, may hold values from -0.5 to 0.5
- lag_picks: int32 [2048, 2048], P('row', 'col'), may hold values from -2 to 2
- pair_valid: int32 [2048, 2048], P('row', 'col'), may hold values 0 or 1
- clock_offset: float32 [2048], P(('row', 'col')), may hold values from -12 to 12
- clock_drift: float32 [2048], P(('row', 'col')), may hold values from -3 to 3
- var_offset: float32 [2048], P(('row', 'col')), may hold values from 0.5 to 2
- cov_cross: float32 [2048], P(('row', 'col')), may hold values from -0.4 to 0.4
- var_drift: float32 [2048], P(('row', 'col')), may hold values from 0.5 to 2
Outputs:
- pair_misfit: float32 [2048, 2048], P('row', 'col')
- new_offset: float32 [2048], P(('row', 'col'))
- new_drift: float32 [2048], P(('row', 'col'))
- new_var_offset: float32 [2048], P(('row', 'col'))
- new_cov_cross: float32 [2048], P(('row', 'col'))
- new_var_drift: float32 [2048], P(('row', 'col'))
All inputs are finite; a program needn't handle non-finite values. No bound on the sum of `pair_valid` on one device may be relied on, other than what follows from the above.
Results may differ from a plain program's by a relative error of at most 0.0008.
Values may be sent and summed in bfloat16 or wider, within the bound.
No kernel may reach another device: no remote copies, remote signals or barrier semaphores. Data moves between devices by JAX's collectives and lax.ppermute only.
A program may use at most 64 MiB of HBM per device.

v0:
```python
import math

import jax
import jax.numpy as jnp
from jax import lax
from jax.sharding import PartitionSpec as P

LAG = 2


EPS = 1e-06
RHO = 0.5
Q_OFFSET = 0.05
Q_DRIFT = 0.01


def whiten(raw_rows, filter_taps):
    signal = raw_rows.astype(jnp.float32)[:, None, :]
    kernel = filter_taps[None, None, :]
    filtered = lax.conv_general_dilated(
        signal,
        kernel,
        (1,),
        "VALID",
        dimension_numbers=("NCH", "OIH", "NCH"),
        precision=lax.Precision.HIGHEST,
    )[:, 0, :]
    scaling = jnp.sqrt(jnp.mean(filtered * filtered, axis=1, keepdims=True) + EPS)
    return (filtered / scaling).astype(jnp.bfloat16)


def fitted_lag(white_rows, column_white, pick_rows):
    window = white_rows.shape[1] - 128
    centre_rows = white_rows[:, 64 : 64 + window]
    before_lag = jnp.zeros(pick_rows.shape, jnp.float32)
    at_lag = jnp.zeros(pick_rows.shape, jnp.float32)
    after_lag = jnp.zeros(pick_rows.shape, jnp.float32)
    for shift in range(-LAG - 1, LAG + 2):
        shifted = column_white[:, 64 + shift : 64 + shift + window]
        correl = lax.dot_general(
            centre_rows, shifted, (((1,), (1,)), ((), ())), preferred_element_type=jnp.float32
        ) / math.sqrt(window)
        before_lag = before_lag + jnp.where(pick_rows - 1 == shift, correl, 0.0)
        at_lag = at_lag + jnp.where(pick_rows == shift, correl, 0.0)
        after_lag = after_lag + jnp.where(pick_rows + 1 == shift, correl, 0.0)
    spread = jnp.maximum(
        jnp.sqrt(before_lag * before_lag + at_lag * at_lag + after_lag * after_lag), 1.0
    )
    return pick_rows.astype(jnp.float32) + (after_lag - before_lag) / spread


def local(
    raw_records,
    filter_taps,
    lag_picks,
    pair_valid,
    clock_offset,
    clock_drift,
    var_offset,
    cov_cross,
    var_drift,
):
    per_device = raw_records.shape[0]
    rows_count = lax.axis_size("row")
    cols_count = lax.axis_size("col")
    stations = per_device * rows_count * cols_count
    offset_pred = clock_offset + clock_drift
    voff = var_offset + 2.0 * cov_cross + var_drift + Q_OFFSET
    vcross = cov_cross + var_drift
    vdrift = var_drift + Q_DRIFT
    everyone = lax.all_gather(offset_pred, ("row", "col"), axis=0, tiled=True)
    offset_grid = everyone.reshape(rows_count, cols_count, per_device)
    row_index = lax.axis_index("row")
    col_index = lax.axis_index("col")
    row_offsets = lax.dynamic_index_in_dim(offset_grid, row_index, 0, keepdims=False).reshape(-1)
    column_offsets = lax.dynamic_index_in_dim(offset_grid, col_index, 1, keepdims=False).reshape(-1)
    valid_float = pair_valid.astype(jnp.float32)
    own_white = whiten(raw_records, filter_taps)
    column_white = lax.all_gather(own_white, "row", axis=0, tiled=True)
    white_rows = lax.all_gather(own_white, "col", axis=0, tiled=True)
    count = white_rows.shape[0]
    pick_rows = lax.slice_in_dim(lag_picks, 0, count, axis=0)
    valid_rows = lax.slice_in_dim(valid_float, 0, count, axis=0)
    offset_rows = lax.slice_in_dim(row_offsets, 0, count, axis=0)
    lagged = fitted_lag(white_rows, column_white, pick_rows)
    pair_misfit = valid_rows * (lagged - offset_rows[:, None] + column_offsets[None, :])
    row_terms = (jnp.sum(pair_misfit, axis=1), jnp.sum(valid_float, axis=1))
    column_terms = (-jnp.sum(pair_misfit, axis=0), jnp.sum(valid_float, axis=0))
    row_whole = lax.psum((row_terms[0], row_terms[1]), "col")
    column_whole = lax.psum((column_terms[0], column_terms[1]), "row")
    row_misfit = lax.dynamic_slice_in_dim(row_whole[0], col_index * per_device, per_device, 0)
    row_pairs = lax.dynamic_slice_in_dim(row_whole[1], col_index * per_device, per_device, 0)
    column_misfit = lax.dynamic_slice_in_dim(column_whole[0], row_index * per_device, per_device, 0)
    column_pairs = lax.dynamic_slice_in_dim(column_whole[1], row_index * per_device, per_device, 0)
    innovation = row_misfit + column_misfit
    pairs = row_pairs + column_pairs
    denom = pairs * voff + RHO * stations
    share = innovation / denom
    new_offset = offset_pred + voff * share
    new_drift = clock_drift + vcross * share
    new_var_offset = voff - voff * voff * pairs / denom
    new_cov_cross = vcross - voff * vcross * pairs / denom
    new_var_drift = vdrift - vcross * vcross * pairs / denom
    return (pair_misfit, new_offset, new_drift, new_var_offset, new_cov_cross, new_var_drift)


def solution(mesh):
    in_specs = (
        P(("row", "col"), None),
        P(),
        P("row", "col"),
        P("row", "col"),
        P(("row", "col")),
        P(("row", "col")),
        P(("row", "col")),
        P(("row", "col")),
        P(("row", "col")),
    )
    out_specs = (
        P("row", "col"),
        P(("row", "col")),
        P(("row", "col")),
        P(("row", "col")),
        P(("row", "col")),
        P(("row", "col")),
    )
    return jax.shard_map(local, mesh=mesh, in_specs=in_specs, out_specs=out_specs, check_vma=False)
```

profile of v0, /device:TPU:1, one launch (start us, length us, event | category | flops | bytes accessed | tf_op | source)
XLA Modules:
  0.0 324.8 jit_solution(12213304597258253916)
XLA Ops:
  0.7 0.6 copy-done.2
  1.3 0.1 fusion.20
  1.4 106.1 %all-reduce = f32[2048]{0:T(1024)S(1)} all-reduce(f32[2048]{0:T(1024)S(1)} %get-tuple-element.19), channel_id=1, replica_groups=mesh['row'=16,'col'=32] {'row','col'}, use_global_device_ids=true, to_apply=%add | all-reduce | flops 2048 | bytes 16384
  107.5 0.3 reshape.27
  107.8 0.1 sub.33
  107.9 0.1 add.174
  108.0 0.6 copy-done.1
  108.6 0.4 copy.20
  109.0 0.7 copy-done.5
  109.7 0.1 copy.21
  109.8 49.0 %fusion.21 = f32[4,1,640]{0,1,2:T(1,128)S(1)} fusion(bf16[4,1,768]{0,1,2:T(2,128)(2,1)S(1)} %copy.20, f32[1,1,129]{1,0,2:T(1,128)S(1)} %copy.21), kind=kOutput, calls=%fused_computation.51 | convolution fusion | flops 3962880 | bytes 16900 | tf_op jit(solution)/shard_map/conv_general_dilated | solution.py:20
  158.8 0.1 multiply_reduce_fusion
  159.0 0.1 copy.22
  159.1 33.0 %all-gather = bf16[32,4,640]{2,1,0:T(4,128)(2,1)S(1)} all-gather(bf16[1,4,640]{2,1,0:T(4,128)(2,1)S(1)} %copy.22), channel_id=1, replica_groups=mesh['row'=16,'col'=32] {'col'}, dimensions={0}, use_global_device_ids=true | all-gather | bytes 168960 | tf_op jit(solution)/shard_map/all_gather | solution.py:80
  192.1 30.2 %all-gather.1 = bf16[16,4,640]{2,1,0:T(4,128)(2,1)S(1)} all-gather(bf16[1,4,640]{2,1,0:T(4,128)(2,1)S(1)} %copy.22), channel_id=1, replica_groups=mesh['row'=16,'col'=32] {'row'}, dimensions={0}, use_global_device_ids=true | all-gather | bytes 87040 | tf_op jit(solution)/shard_map/all_gather | solution.py:79
  222.3 0.2 convolution_multiply_fusion.6
  222.6 0.3 convolution_multiply_fusion.5
  222.8 0.3 convolution_multiply_fusion.4
  223.1 0.3 convolution_multiply_fusion.3
  223.3 0.3 convolution_multiply_fusion.2
  223.6 0.2 convolution_multiply_fusion.1
  223.8 0.5 copy-done
  224.3 0.0 copy-done.8
  224.4 1.0 fusion.19
  225.4 0.1 convert_reduce_fusion.1
  225.5 30.2 %all-reduce.2 = (f32[64]{0:T(128)S(1)}, f32[64]{0:T(128)S(1)}) all-reduce(f32[64]{0:T(128)S(1)} %neg.3, f32[64]{0:T(128)S(1)} %get-tuple-element.7), channel_id=1, replica_groups=mesh['row'=16,'col'=32] {'row'}, use_global_device_ids=true, to_apply=%region_4.5 | all-reduce | flops 128 | bytes 1024 | tf_op jit(solution)/shard_map/psum | solution.py:90
  255.7 66.7 %all-reduce.1 = (f32[128]{0:T(128)S(1)}, f32[128]{0:T(128)S(1)}) all-reduce(f32[128]{0:T(128)S(1)} %get-tuple-element.8, f32[128]{0:T(128)S(1)} %get-tuple-element.6), channel_id=1, replica_groups=mesh['row'=16,'col'=32] {'col'}, use_global_device_ids=true, to_apply=%region_2.3 | all-reduce | flops 256 | bytes 2048 | tf_op jit(solution)/shard_map/psum | solution.py:89
  322.4 0.6 copy-done.3
  323.1 0.0 copy-done.7
  323.1 0.6 divide_subtract_fusion
  323.7 0.6 multiply_add_fusion
  324.3 0.5 multiply_add_fusion.1
  (19 shorter events, 0.2 us)
Async XLA Ops:
  0.6 0.7 copy-start.2
  0.7 0.7 copy-start.6
  107.9 0.7 copy-start.1
  109.0 0.7 copy-start.5
  223.6 0.8 copy-start
  223.6 0.8 copy-start.8
  322.4 0.7 copy-start.3
  322.4 0.7 copy-start.4
  322.4 0.7 copy-start.7
where the time goes:
time: 325 us
  blocking collectives  266 us (82%)
  matrix products  51.5 us (16%)
  local copies, waits for them, and re-layouts  4.3 us (1%)
    unnamed x1, blocking collectives  106 us
    psum x1, blocking collectives, local(): row_whole = lax.psum((row_terms[0], row_terms[1]), 'col')  66.7 us
    conv_general_dilated x1, matrix products, whiten(): lax.conv_general_dilated(signal, kernel, (1,), 'VALID', dimension_numbers...  49 us
    all_gather x1, blocking collectives, local(): white_rows = lax.all_gather(own_white, 'col', axis=0, tiled=True)  33 us
    all_gather x1, blocking collectives, local(): column_white = lax.all_gather(own_white, 'row', axis=0, tiled=True)  30.2 us
    psum x1, blocking collectives, local(): column_whole = lax.psum((column_terms[0], column_terms[1]), 'row')  30.2 us

commit v1 on v0

v1 whole, which is shorter than its diff:
```python
import math

import jax
import jax.numpy as jnp
from jax import lax
from jax.experimental import pallas as pl
from jax.experimental.pallas import tpu as pltpu
from jax.sharding import PartitionSpec as P

LAG = 2

EPS = 1e-06
RHO = 0.5
Q_OFFSET = 0.05
Q_DRIFT = 0.01

LANES = 128
OFF_LANE = 8

NT = (((1,), (1,)), ((), ()))


def three_terms(values):
    hi = values.astype(jnp.bfloat16)
    rest = values - hi.astype(jnp.float32)
    mid = rest.astype(jnp.bfloat16)
    low = (rest - mid.astype(jnp.float32)).astype(jnp.bfloat16)
    return hi, mid, low


def lane_index(shape):
    return lax.broadcasted_iota(jnp.int32, shape, 1)


def whiten_kernel(raw_ref, taps_ref, offset_ref, drift_ref, voff_ref, cross_ref, vdrift_ref,
                  row_ref, column_ref, state_ref, taps_pad):
    stations, samples = raw_ref.shape
    taps = taps_ref.shape[1]
    blocks = (samples - taps + 1) // LANES
    taps_pad[...] = jnp.zeros_like(taps_pad)
    taps_pad[0:1, 0:taps] = taps_ref[...]
    spread_taps = jnp.broadcast_to(taps_pad[0:1, :], (LANES, 2 * LANES))
    band = pltpu.roll(spread_taps, 0, 1, stride=1, stride_axis=0)
    bands = jnp.concatenate(three_terms(band), axis=0)
    raw = raw_ref[...].astype(jnp.float32)
    pieces = jnp.concatenate(
        [raw[:, b * LANES : (b + 2) * LANES] for b in range(blocks)], axis=0
    ).astype(jnp.bfloat16)
    terms = lax.dot_general(pieces, bands, NT, preferred_element_type=jnp.float32)
    filtered = terms[:, :LANES] + (terms[:, LANES : 2 * LANES] + terms[:, 2 * LANES :])
    parts = [filtered[b * stations : (b + 1) * stations] for b in range(blocks)]
    squares = parts[0] * parts[0]
    for part in parts[1:]:
        squares = squares + part * part
    mean = jnp.sum(squares, axis=1, keepdims=True) / (blocks * LANES)
    scaling = jnp.sqrt(mean + EPS)
    turned = [pltpu.roll(part / scaling, LANES // 2, 1) for part in parts]
    lane = lane_index((stations, LANES))
    rolled = [
        jnp.where(lane < LANES // 2, turned[b], turned[(b + 1) % blocks]) for b in range(blocks)
    ]
    offset_pred = offset_ref[...] + drift_ref[...]
    square = (stations, stations)
    diagonal = lax.broadcasted_iota(jnp.int32, square, 0) == lane_index(square)
    standing = jnp.sum(
        jnp.where(diagonal, jnp.broadcast_to(offset_pred, square), 0.0), axis=1, keepdims=True
    )
    for k, term in enumerate(three_terms(standing)):
        rolled[-1] = jnp.where(lane == OFF_LANE + k, term.astype(jnp.float32), rolled[-1])
    row = jnp.concatenate(rolled, axis=1).astype(jnp.bfloat16)
    for ref in (row_ref, column_ref):
        for peer in range(ref.shape[0]):
            ref[peer] = row
    cross = cross_ref[...]
    vdrift = vdrift_ref[...]
    state_ref[0:1, 0:stations] = offset_pred
    state_ref[1:2, 0:stations] = drift_ref[...]
    state_ref[2:3, 0:stations] = voff_ref[...] + 2.0 * cross + vdrift + Q_OFFSET
    state_ref[3:4, 0:stations] = cross + vdrift
    state_ref[4:5, 0:stations] = vdrift + Q_DRIFT


def pair_kernel(rows_ref, columns_ref, picks_ref, valid_ref,
                misfit_ref, row_sums_ref, column_sums_ref):
    count, width = columns_ref.shape
    window = width - LANES
    columns = columns_ref[...].astype(jnp.float32)
    shifts = range(-LAG - 1, LAG + 2)
    shifted = [
        (columns if shift == 0 else pltpu.roll(columns, (-shift) % width, 1))[:, :window]
        for shift in shifts
    ]
    stacked = jnp.concatenate(shifted, axis=0).astype(jnp.bfloat16)
    products = lax.dot_general(
        stacked, rows_ref[:, :window], NT, preferred_element_type=jnp.float32
    ) * (1.0 / math.sqrt(window))
    correl = {
        shift: products[k * count : (k + 1) * count] for k, shift in enumerate(shifts)
    }
    picks = picks_ref[...]
    shape = picks.shape
    before_lag = jnp.zeros(shape, jnp.float32)
    at_lag = before_lag
    after_lag = before_lag
    for pick in range(-LAG, LAG + 1):
        here = picks == pick
        before_lag = jnp.where(here, correl[pick - 1], before_lag)
        at_lag = jnp.where(here, correl[pick], at_lag)
        after_lag = jnp.where(here, correl[pick + 1], after_lag)
    spread = jnp.maximum(
        jnp.sqrt(before_lag * before_lag + at_lag * at_lag + after_lag * after_lag), 1.0
    )
    lagged = picks.astype(jnp.float32) + (after_lag - before_lag) / spread

    def holds_offset(lane):
        return (lane >= OFF_LANE) & (lane < OFF_LANE + 3)

    picker = jnp.where(holds_offset(lane_index((8, LANES))), 1.0, 0.0).astype(jnp.bfloat16)
    row_offsets = lax.dot_general(
        picker, rows_ref[:, window:], NT, preferred_element_type=jnp.float32
    )[0:1]
    tail = columns[:, window:]
    column_offsets = jnp.sum(
        jnp.where(holds_offset(lane_index(tail.shape)), tail, 0.0), axis=1, keepdims=True
    )
    valid = valid_ref[...].astype(jnp.float32)
    misfit = valid * (lagged - row_offsets + column_offsets)
    misfit_ref[...] = misfit
    rows = (jnp.sum(values, axis=0, keepdims=True) for values in (misfit, valid))
    row_sums_ref[...] = jnp.broadcast_to(
        jnp.concatenate(list(rows), axis=0)[None], row_sums_ref.shape
    )
    lane = lane_index(shape)
    station = lax.broadcasted_iota(jnp.int32, shape, 0)
    sums, counts = (jnp.sum(values, axis=1, keepdims=True) for values in (misfit, valid))
    laid = jnp.where(lane == station, sums, jnp.where(lane == station + count, counts, 0.0))
    column_sums_ref[...] = jnp.broadcast_to(
        jnp.sum(laid, axis=0, keepdims=True), column_sums_ref.shape
    )


def update_kernel(whole, row_sums_ref, column_sums_ref, state_ref,
                  offset_ref, drift_ref, voff_ref, cross_ref, vdrift_ref):
    stations = offset_ref.shape[1]
    rows = jnp.sum(row_sums_ref[...], axis=0)
    columns = jnp.sum(column_sums_ref[...], axis=0, keepdims=True)
    row_start = lax.axis_index("col") * stations
    column_start = lax.axis_index("row") * stations
    in_column = LANES // 2

    def from_lane(line, start):
        return pltpu.roll(line, lax.rem(LANES - start, LANES), 1)[:, :stations]

    innovation = from_lane(rows[0:1], row_start) - from_lane(columns, column_start)
    pairs = from_lane(rows[1:2], row_start) + from_lane(columns, column_start + in_column)
    offset_pred, drift, voff, vcross, vdrift = (
        state_ref[k : k + 1, 0:stations] for k in range(5)
    )
    denom = pairs * voff + RHO * whole
    share = innovation / denom
    offset_ref[...] = offset_pred + voff * share
    drift_ref[...] = drift + vcross * share
    voff_ref[...] = voff - voff * voff * pairs / denom
    cross_ref[...] = vcross - voff * vcross * pairs / denom
    vdrift_ref[...] = vdrift - vcross * vcross * pairs / denom


def in_vmem(count):
    return [pl.BlockSpec(memory_space=pltpu.VMEM)] * count


def pinned(*arrays):
    return [pltpu.with_memory_space_constraint(array, pltpu.VMEM) for array in arrays]


def local(
    raw_records,
    filter_taps,
    lag_picks,
    pair_valid,
    clock_offset,
    clock_drift,
    var_offset,
    cov_cross,
    var_drift,
):
    stations, samples = raw_records.shape
    rows_count = lax.axis_size("row")
    cols_count = lax.axis_size("col")
    taps = filter_taps.shape[0]
    width = samples - taps + 1
    in_row = stations * cols_count
    in_column = stations * rows_count
    line = (1, stations)
    for_rows, for_columns, state = pl.pallas_call(
        whiten_kernel,
        out_shape=(
            pltpu.VMEM((cols_count, stations, width), jnp.bfloat16),
            pltpu.VMEM((rows_count, stations, width), jnp.bfloat16),
            pltpu.VMEM((8, LANES), jnp.float32),
        ),
        in_specs=in_vmem(7),
        out_specs=tuple(in_vmem(3)),
        scratch_shapes=[pltpu.VMEM((8, 2 * LANES), jnp.float32)],
        name="whiten",
    )(
        raw_records,
        filter_taps.reshape(1, taps),
        clock_offset.reshape(line),
        clock_drift.reshape(line),
        var_offset.reshape(line),
        cov_cross.reshape(line),
        var_drift.reshape(line),
    )
    white_rows = lax.all_to_all(for_rows, "col", 0, 0, tiled=True).reshape(in_row, width)
    white_rows, for_columns = lax.optimization_barrier((white_rows, for_columns))
    white_columns = lax.all_to_all(for_columns, "row", 0, 0, tiled=True).reshape(in_column, width)
    misfit, row_sums, column_sums = pl.pallas_call(
        pair_kernel,
        out_shape=(
            jax.ShapeDtypeStruct((in_column, in_row), jnp.float32),
            pltpu.VMEM((cols_count, 2, LANES), jnp.float32),
            pltpu.VMEM((rows_count, LANES), jnp.float32),
        ),
        in_specs=in_vmem(4),
        out_specs=tuple(in_vmem(3)),
        name="pairs",
    )(*pinned(white_rows, white_columns, lag_picks.T, pair_valid.T))
    row_sums = lax.all_to_all(row_sums, "col", 0, 0, tiled=True)
    column_sums = lax.all_to_all(column_sums, "row", 0, 0, tiled=True)
    whole = stations * rows_count * cols_count
    updated = pl.pallas_call(
        lambda *refs: update_kernel(whole, *refs),
        out_shape=tuple(jax.ShapeDtypeStruct(line, jnp.float32) for _ in range(5)),
        in_specs=in_vmem(3),
        out_specs=tuple(in_vmem(5)),
        name="update",
    )(*pinned(row_sums, column_sums, state))
    return (misfit.T,) + tuple(values.reshape(stations) for values in updated)


def solution(mesh):
    in_specs = (
        P(("row", "col"), None),
        P(),
        P("row", "col"),
        P("row", "col"),
        P(("row", "col")),
        P(("row", "col")),
        P(("row", "col")),
        P(("row", "col")),
        P(("row", "col")),
    )
    out_specs = (
        P("row", "col"),
        P(("row", "col")),
        P(("row", "col")),
        P(("row", "col")),
        P(("row", "col")),
        P(("row", "col")),
    )
    return jax.shard_map(local, mesh=mesh, in_specs=in_specs, out_specs=out_specs, check_vma=False)
```

time: 325 us -> 70.3 us (0.22)
  blocking collectives: 266 us -> 65.7 us
  matrix products: 51.5 us -> 0 us
  local copies, waits for them, and re-layouts: 4.3 us -> 0.81 us
    unnamed x1 -> x0, blocking collectives: 106 us -> none
    psum x2 -> x0, blocking collectives: 96.9 us -> none  [the longest x1 66.7 us: local(): row_whole = lax.psum((row_terms[0], row_terms[1]), 'col')]
    all_to_all x0 -> x4, blocking collectives: none -> 65.7 us  [the longest x1 21 us: local(): lax.all_to_all(for_columns, 'row', 0, 0, tiled=True)]
    all_gather x2 -> x0, blocking collectives: 63.2 us -> none  [the longest x1 33 us: local(): white_rows = lax.all_gather(own_white, 'col', axis=0, tiled=True)]
    conv_general_dilated x1 -> x0, matrix products: 49 us -> none  [whiten(): lax.conv_general_dilated(signal, kernel, (1,), 'VALID', dimension_numbers...]
where the time goes in v1:
time: 70.3 us; the launch traced here: 70 us
  blocking collectives  65.7 us (93%)
  Pallas kernels  2.83 us (4%)
  local copies, waits for them, and re-layouts  0.81 us (1%)
    all_to_all x1, blocking collectives, local(): lax.all_to_all(for_columns, 'row', 0, 0, tiled=True)  21 us
    all_to_all x1, blocking collectives, local(): lax.all_to_all(for_rows, 'col', 0, 0, tiled=True).reshape(in_row, width)  19.4 us
    all_to_all x1, blocking collectives, local(): row_sums = lax.all_to_all(row_sums, 'col', 0, 0, tiled=True)  13.9 us
    all_to_all x1, blocking collectives, local(): column_sums = lax.all_to_all(column_sums, 'row', 0, 0, tiled=True)  11.4 us

profile of v1, /device:TPU:1, one launch (start us, length us, event | category | flops | bytes accessed | tf_op | source)
XLA Modules:
  0.0 70.0 jit_solution(6868758606886841204)
XLA Ops:
  0.6 1.2 %whiten.1 = (bf16[32,4,640]{2,1,0:T(4,128)(2,1)S(1)}, bf16[16,4,640]{2,1,0:T(4,128)(2,1)S(1)}, f32[8,128]{1,0:T(8,128)S(1)}) custom-call(bf16[4,768]{1,0:T(4,128)(2,1)} %raw_ref.1, f32[1,129]{1,0:T(1,128)} %bitcast.22, f32[1,4]{1,0:T(1,128)} %bitcast.23, f32[1,4]{1,0:T(1,128)} %bitcast.24, f32[1,4]{1,0:T(1,128)} %bitcast.25, f32[1,4]{1,0:T(1,128)} %bitcast.26, ...), custom_call_target="tpu_custom_call" | custom-call | tf_op jit(solution)/shard_map/whiten/pallas_call | solution.py:195
  1.9 19.4 %all_to_all.26 = bf16[32,4,640]{2,1,0:T(4,128)(2,1)S(1)} all-to-all(bf16[32,4,640]{2,1,0:T(4,128)(2,1)S(1)} %get-tuple-element.19), channel_id=1, replica_groups=mesh['row'=16,'col'=32] {'col'}, dimensions={0} | all-to-all | bytes 327680 | tf_op jit(solution)/shard_map/all_to_all | solution.py:215
  21.3 21.0 %all_to_all.27 = bf16[16,4,640]{2,1,0:T(4,128)(2,1)S(1)} all-to-all(bf16[16,4,640]{2,1,0:T(4,128)(2,1)S(1)} %get-tuple-element.22), channel_id=1, replica_groups=mesh['row'=16,'col'=32] {'row'}, dimensions={0} | all-to-all | bytes 163840 | tf_op jit(solution)/shard_map/all_to_all | solution.py:217
  42.2 0.0 copy-start
  42.2 0.0 copy-start.1
  42.3 0.7 %copy-done = s32[128,64]{0,1:T(8,128)S(1)} copy-done((s32[128,64]{0,1:T(8,128)S(1)}, s32[128,64]{0,1:T(8,128)}, u32[]{:S(2)}) %copy-start) | copy-done | bytes 32792
  43.0 0.0 copy-done.1
  43.0 1.0 %pairs.1 = (f32[64,128]{1,0:T(8,128)}, f32[32,2,128]{2,1,0:T(2,128)S(1)}, f32[16,128]{1,0:T(8,128)S(1)}) custom-call(bf16[128,640]{1,0:T(8,128)(2,1)S(1)} %reshape.59.rows_ref, bf16[64,640]{1,0:T(8,128)(2,1)S(1)} %reshape.60.columns_ref, s32[64,128]{1,0:T(8,128)S(1)} %bitcast.18, s32[64,128]{1,0:T(8,128)S(1)} %bitcast.19), custom_call_target="tpu_custom_call" | custom-call | tf_op jit(solution)/shard_map/pairs/pallas_call | solution.py:218
  44.0 11.4 %all_to_all.28 = f32[16,1,128]{2,1,0:T(1,128)S(1)} all-to-all(f32[16,1,128]{2,1,0:T(1,128)S(1)} %bitcast.21), channel_id=1, replica_groups=mesh['row'=16,'col'=32] {'row'}, dimensions={0} | all-to-all | bytes 16384 | tf_op jit(solution)/shard_map/all_to_all | solution.py:230
  55.4 13.9 %all_to_all.29.refs_0_ = f32[32,2,128]{2,1,0:T(2,128)S(1)} all-to-all(f32[32,2,128]{2,1,0:T(2,128)S(1)} %get-tuple-element.24), channel_id=1, replica_groups=mesh['row'=16,'col'=32] {'col'}, dimensions={0} | all-to-all | bytes 65536 | tf_op jit(solution)/shard_map/all_to_all | solution.py:229
  69.3 0.6 update.1
  (2 shorter events, 0.1 us)
Async XLA Ops:
  42.2 0.8 %copy-start = (s32[128,64]{0,1:T(8,128)S(1)}, s32[128,64]{0,1:T(8,128)}, u32[]{:S(2)}) copy-start(s32[128,64]{0,1:T(8,128)} %param.11) | copy-start | bytes 98308
  42.2 0.8 %copy-start.1 = (s32[128,64]{0,1:T(8,128)S(1)}, s32[128,64]{0,1:T(8,128)}, u32[]{:S(2)}) copy-start(s32[128,64]{0,1:T(8,128)} %param.12) | copy-start | bytes 98308

commit v2 on v1

--- a/solution.py
+++ b/solution.py
@@ -33,7 +33,8 @@
 
 
 def whiten_kernel(raw_ref, taps_ref, offset_ref, drift_ref, voff_ref, cross_ref, vdrift_ref,
-                  row_ref, column_ref, state_ref, taps_pad):
+                  picks_ref, valid_ref,
+                  row_ref, column_ref, state_ref, near_picks_ref, near_valid_ref, taps_pad):
     stations, samples = raw_ref.shape
     taps = taps_ref.shape[1]
     blocks = (samples - taps + 1) // LANES
@@ -78,6 +79,8 @@
     state_ref[2:3, 0:stations] = voff_ref[...] + 2.0 * cross + vdrift + Q_OFFSET
     state_ref[3:4, 0:stations] = cross + vdrift
     state_ref[4:5, 0:stations] = vdrift + Q_DRIFT
+    near_picks_ref[...] = picks_ref[...]
+    near_valid_ref[...] = valid_ref[...].astype(jnp.float32)
 
 
 def pair_kernel(rows_ref, columns_ref, picks_ref, valid_ref,
@@ -123,7 +126,7 @@
     column_offsets = jnp.sum(
         jnp.where(holds_offset(lane_index(tail.shape)), tail, 0.0), axis=1, keepdims=True
     )
-    valid = valid_ref[...].astype(jnp.float32)
+    valid = valid_ref[...]
     misfit = valid * (lagged - row_offsets + column_offsets)
     misfit_ref[...] = misfit
     rows = (jnp.sum(values, axis=0, keepdims=True) for values in (misfit, valid))
@@ -139,8 +142,9 @@
     )
 
 
-def update_kernel(whole, row_sums_ref, column_sums_ref, state_ref,
-                  offset_ref, drift_ref, voff_ref, cross_ref, vdrift_ref):
+def update_kernel(whole, row_sums_ref, column_sums_ref, state_ref, near_misfit_ref,
+                  misfit_ref, offset_ref, drift_ref, voff_ref, cross_ref, vdrift_ref):
+    misfit_ref[...] = near_misfit_ref[...]
     stations = offset_ref.shape[1]
     rows = jnp.sum(row_sums_ref[...], axis=0)
     columns = jnp.sum(column_sums_ref[...], axis=0, keepdims=True)
@@ -192,15 +196,18 @@
     in_row = stations * cols_count
     in_column = stations * rows_count
     line = (1, stations)
-    for_rows, for_columns, state = pl.pallas_call(
+    block = (in_column, in_row)
+    for_rows, for_columns, state, picks, valid = pl.pallas_call(
         whiten_kernel,
         out_shape=(
             pltpu.VMEM((cols_count, stations, width), jnp.bfloat16),
             pltpu.VMEM((rows_count, stations, width), jnp.bfloat16),
             pltpu.VMEM((8, LANES), jnp.float32),
+            pltpu.VMEM(block, jnp.int32),
+            pltpu.VMEM(block, jnp.float32),
         ),
-        in_specs=in_vmem(7),
-        out_specs=tuple(in_vmem(3)),
+        in_specs=in_vmem(9),
+        out_specs=tuple(in_vmem(5)),
         scratch_shapes=[pltpu.VMEM((8, 2 * LANES), jnp.float32)],
         name="whiten",
     )(
@@ -211,6 +218,8 @@
         var_offset.reshape(line),
         cov_cross.reshape(line),
         var_drift.reshape(line),
+        lag_picks.T,
+        pair_valid.T,
     )
     white_rows = lax.all_to_all(for_rows, "col", 0, 0, tiled=True).reshape(in_row, width)
     white_rows, for_columns = lax.optimization_barrier((white_rows, for_columns))
@@ -218,24 +227,24 @@
     misfit, row_sums, column_sums = pl.pallas_call(
         pair_kernel,
         out_shape=(
-            jax.ShapeDtypeStruct((in_column, in_row), jnp.float32),
+            pltpu.VMEM(block, jnp.float32),
             pltpu.VMEM((cols_count, 2, LANES), jnp.float32),
             pltpu.VMEM((rows_count, LANES), jnp.float32),
         ),
         in_specs=in_vmem(4),
         out_specs=tuple(in_vmem(3)),
         name="pairs",
-    )(*pinned(white_rows, white_columns, lag_picks.T, pair_valid.T))
+    )(*pinned(white_rows, white_columns, picks, valid))
     row_sums = lax.all_to_all(row_sums, "col", 0, 0, tiled=True)
     column_sums = lax.all_to_all(column_sums, "row", 0, 0, tiled=True)
     whole = stations * rows_count * cols_count
-    updated = pl.pallas_call(
+    misfit, *updated = pl.pallas_call(
         lambda *refs: update_kernel(whole, *refs),
-        out_shape=tuple(jax.ShapeDtypeStruct(line, jnp.float32) for _ in range(5)),
-        in_specs=in_vmem(3),
-        out_specs=tuple(in_vmem(5)),
+        out_shape=tuple(jax.ShapeDtypeStruct(shape, jnp.float32) for shape in (block,) + (line,) * 5),
+        in_specs=in_vmem(4),
+        out_specs=tuple(in_vmem(6)),
         name="update",
-    )(*pinned(row_sums, column_sums, state))
+    )(*pinned(row_sums, column_sums, state, misfit))
     return (misfit.T,) + tuple(values.reshape(stations) for values in updated)
 
 

time: 70.3 us -> 69.1 us (0.983)
  local copies, waits for them, and re-layouts: 0.81 us -> 0.07 us
    unnamed x4 -> x0, local copies, waits for them, and re-layouts: 0.75 us -> none
where the time goes in v2:
time: 69.1 us; the launch traced here: 68.8 us
  blocking collectives  65.7 us (95%)
  Pallas kernels  2.44 us (4%)
    all_to_all x1, blocking collectives, local(): lax.all_to_all(for_columns, 'row', 0, 0, tiled=True)  21 us
    all_to_all x1, blocking collectives, local(): lax.all_to_all(for_rows, 'col', 0, 0, tiled=True).reshape(in_row, width)  19.4 us
    all_to_all x1, blocking collectives, local(): row_sums = lax.all_to_all(row_sums, 'col', 0, 0, tiled=True)  13.9 us
    all_to_all x1, blocking collectives, local(): column_sums = lax.all_to_all(column_sums, 'row', 0, 0, tiled=True)  11.4 us

profile of v2, /device:TPU:1, one launch (start us, length us, event | category | flops | bytes accessed | tf_op | source)
XLA Modules:
  0.0 68.8 jit_solution(3816766060537108463)
XLA Ops:
  0.6 1.4 %whiten.1 = (bf16[32,4,640]{2,1,0:T(4,128)(2,1)S(1)}, bf16[16,4,640]{2,1,0:T(4,128)(2,1)S(1)}, f32[8,128]{1,0:T(8,128)S(1)}, s32[64,128]{1,0:T(8,128)S(1)}, f32[64,128]{1,0:T(8,128)S(1)}) custom-call(bf16[4,768]{1,0:T(4,128)(2,1)} %raw_ref.1, f32[1,129]{1,0:T(1,128)} %bitcast.22, f32[1,4]{1,0:T(1,128)} %bitcast.23, f32[1,4]{1,0:T(1,128)} %bitcast.24, ...), custom_call_target="tpu_custom_call" | custom-call | tf_op jit(solution)/shard_map/whiten/pallas_call | solution.py:200
  2.0 19.4 %all_to_all.26 = bf16[32,4,640]{2,1,0:T(4,128)(2,1)S(1)} all-to-all(bf16[32,4,640]{2,1,0:T(4,128)(2,1)S(1)} %get-tuple-element.22), channel_id=1, replica_groups=mesh['row'=16,'col'=32] {'col'}, dimensions={0} | all-to-all | bytes 327680 | tf_op jit(solution)/shard_map/all_to_all | solution.py:224
  21.4 21.0 %all_to_all.27 = bf16[16,4,640]{2,1,0:T(4,128)(2,1)S(1)} all-to-all(bf16[16,4,640]{2,1,0:T(4,128)(2,1)S(1)} %get-tuple-element.25), channel_id=1, replica_groups=mesh['row'=16,'col'=32] {'row'}, dimensions={0} | all-to-all | bytes 163840 | tf_op jit(solution)/shard_map/all_to_all | solution.py:226
  42.4 0.4 pairs.1
  42.9 11.4 %all_to_all.28 = f32[16,1,128]{2,1,0:T(1,128)S(1)} all-to-all(f32[16,1,128]{2,1,0:T(1,128)S(1)} %bitcast.19), channel_id=1, replica_groups=mesh['row'=16,'col'=32] {'row'}, dimensions={0} | all-to-all | bytes 16384 | tf_op jit(solution)/shard_map/all_to_all | solution.py:239
  54.3 13.9 %all_to_all.29.refs_0_ = f32[32,2,128]{2,1,0:T(2,128)S(1)} all-to-all(f32[32,2,128]{2,1,0:T(2,128)S(1)} %get-tuple-element.28), channel_id=1, replica_groups=mesh['row'=16,'col'=32] {'col'}, dimensions={0} | all-to-all | bytes 65536 | tf_op jit(solution)/shard_map/all_to_all | solution.py:238
  68.2 0.6 update.1
  (2 shorter events, 0.1 us)
